TPU v7x, 32 devices: a whole 2x2x4 slice. The times are simulated.
32 devices in a mesh: row: 4 (over z), col: 4 (over y, x), layer: 2 (over core).
Axes of the slice: x: 2, y: 2, z: 4, core: 2. Of those that a mesh axis runs over, the one named last changes fastest.
Arguments:
- expression: bfloat16 [6144, 1024], P(('row', 'col'), 'layer'), may hold values from -240 to 240
Outputs:
- connectivity: float32 [6144], P(('row', 'col', 'layer'))
All inputs are finite; a program needn't handle non-finite values.
Results may differ from a plain program's by a relative error of at most 0.00048.
Values may be sent and summed in bfloat16 or wider, within the bound.
A program may use at most 64 MiB of HBM per device.

v0:
```python
import jax
import jax.numpy as jnp
from jax import lax
from jax.sharding import PartitionSpec as P

S = 1024


epsilon = 1e-05


def adjacency(correlation):
    shifted = (1.0 + correlation) * 0.5
    square = shifted * shifted
    fourth = square * square
    eighth = fourth * fourth
    return eighth * fourth


def standardize(values, total, squares):
    average = total / S
    variance = squares / S - average * average
    return ((values - average[:, None]) * lax.rsqrt(variance + epsilon)[:, None]).astype(
        jnp.bfloat16
    )


def pair_products(left, right):
    return lax.dot_general(
        left, right, (((1,), (1,)), ((), ())), preferred_element_type=jnp.float32
    )


def on_device(expression):
    whole = lax.all_gather(expression, "layer", axis=1, tiled=True)
    values = whole.astype(jnp.float32)
    scaled = standardize(values, jnp.sum(values, axis=1), jnp.sum(values * values, axis=1))
    row_genes = lax.all_gather(scaled, "col", axis=0, tiled=True)
    share = scaled.shape[0] // lax.axis_size("layer")
    own_half = lax.dynamic_slice_in_dim(scaled, lax.axis_index("layer") * share, share, 0)
    partial_value = jnp.sum(
        adjacency(
            pair_products(lax.all_gather(own_half, "row", axis=0, tiled=True), row_genes) / S
        ),
        axis=0,
    )
    summed = lax.psum_scatter(partial_value, ("col", "layer"), scatter_dimension=0, tiled=True)
    return summed - 1.0


def solution(mesh):
    placed = (P(("row", "col"), "layer"),)
    return jax.shard_map(
        on_device, mesh=mesh, in_specs=placed, out_specs=P(("row", "col", "layer")), check_vma=False
    )
```

profile of v0, /device:TPU:0, one launch (start us, length us, event | category | flops | bytes accessed | tf_op | source)
XLA Modules:
  0.0 121.1 jit_solution(8612865280336026909)
XLA Ops:
  6.5 0.0 copy-start.1
  6.5 0.0 all-gather.3.cloned.1.call-start
  6.5 2.8 %all_gather.9 = bf16[384,1024]{1,0:T(8,128)(2,1)S(1)} all-gather(bf16[384,512]{1,0:T(8,128)(2,1)} %param.1), channel_id=1, replica_groups=mesh['row'=4,'col'=4,'layer'=2] {'layer'}, dimensions={1}, use_global_device_ids=true | all-gather | bytes 1179648 | tf_op jit(solution)/shard_map/all_gather | solution.py:35
  9.4 0.3 convert_reduce_fusion
  9.7 0.3 fusion.2
  9.9 0.0 copy-start
  10.0 0.9 constant_dynamic-slice_fusion
  10.8 0.0 all-gather.3.cloned.1.call-update
  10.8 0.0 all-gather.5.cloned.1.call-start
  10.9 0.1 copy-done
  11.0 0.6 all-gather.5.cloned.1.call-update
  11.6 0.0 copy-done.1
  11.6 0.6 dynamic-slice
  12.8 37.8 %all-gather.3.cloned.1.call-done = bf16[768,1024]{1,0:T(8,128)(2,1)} async-done(((bf16[192,1024]{1,0:T(8,128)(2,1)}), bf16[768,1024]{1,0:T(8,128)(2,1)}) %all-gather.3.cloned.1.call-update) | async-done | bytes 1572880 | tf_op jit(solution)/shard_map/all_gather | solution.py:43
  50.6 44.6 %all-gather.5.cloned.1.call-done = bf16[1536,1024]{1,0:T(8,128)(2,1)} async-done(((bf16[384,1024]{1,0:T(8,128)(2,1)}), bf16[1536,1024]{1,0:T(8,128)(2,1)}) %all-gather.5.cloned.1.call-update) | async-done | bytes 3145744 | tf_op jit(solution)/shard_map/all_gather | solution.py:38
  95.2 5.6 %fusion = f32[1536]{0:T(1024)S(1)} fusion(bf16[768,1024]{1,0:T(8,128)(2,1)} %all-gather.3.cloned.1.call-done, bf16[1536,1024]{1,0:T(8,128)(2,1)} %all-gather.5.cloned.1.call-done), kind=kOutput, calls=%fused_computation.1 | convolution fusion | flops 2425354752 | bytes 4724736 | tf_op jit(solution)/shard_map/dot_general | solution.py:29
  100.8 12.8 %all-reduce = f32[1536]{0:T(1024)S(1)} all-reduce(f32[1536]{0:T(1024)S(1)} %fusion), channel_id=2, replica_groups=mesh['row'=4,'col'=4,'layer'=2] {'col','layer'}, use_global_device_ids=true, to_apply=%region_3.0.clone | all-reduce | flops 1536 | bytes 12288
  113.6 0.6 dynamic-slice_add_fusion
  (1 shorter events, 0.0 us)
Async XLA Ops:
  6.5 5.1 %copy-start.1 = (u32[32]{0:T(128)S(1)}, u32[32]{0:T(128)}, u32[]{:S(2)}) copy-start(u32[32]{0:T(128)} %constant.29) | copy-start | bytes 388
  6.5 44.1 %all-gather.3.cloned.1.call-start = ((), (), s32[]{:S(2)}) async-start(), calls=%async_computation | async-start | bytes 1966080 | tf_op jit(solution)/shard_map/all_gather | solution.py:43
  9.9 1.1 copy-start
  10.8 84.4 %all-gather.5.cloned.1.call-start = ((), (), s32[]{:S(2)}) async-start(), calls=%async_computation.1 | async-start | bytes 3932160 | tf_op jit(solution)/shard_map/all_gather | solution.py:38
Sparse Core Ops, SparseCore 0:
  11.0 39.6 all-gather.2
  52.5 42.6 all-gather.4
where the time goes:
time: 121 us
  waiting for transfers between devices  83 us (69%)
  blocking collectives  15.6 us (13%)
  between operations  14.1 us (12%)
  matrix products  5.59 us (5%)
  local copies, waits for them, and re-layouts  1.56 us (1%)
  other arithmetic  1.22 us (1%)
    all_gather x1, waiting for transfers between devices, on_device(): row_genes = lax.all_gather(scaled, 'col', axis=0, tiled=True)  44.6 us
    all_gather x1, waiting for transfers between devices, on_device(): lax.all_gather(own_half, 'row', axis=0, tiled=True)  37.8 us
    unnamed x1, blocking collectives  12.8 us
    dot_general x1, matrix products, pair_products(): lax.dot_general(left, right, (((1,), (1,)), ((), ())), preferred_element_...  5.59 us
    all_gather x1, blocking collectives, on_device(): whole = lax.all_gather(expression, 'layer', axis=1, tiled=True)  2.82 us
  transfers between devices with their start and end apart: 2, of which 2 were waited for; matrix products, arithmetic and copies ran while one was open for 0% of the time, Pallas kernels for 0%

commit v1 on v0

v1 whole, which is shorter than its diff:
```python
import functools

import jax
import jax.numpy as jnp
from jax import lax
from jax.experimental import pallas as pl
from jax.experimental.pallas import tpu as pltpu
from jax.sharding import PartitionSpec as P

MESH = pl.DeviceIdType.MESH
epsilon = 1e-05


def flip(c, k):
    bit = 1
    while bit <= k:
        if k & bit:
            c = c + bit - 2 * bit * lax.rem(lax.div(c, bit), 2)
        bit *= 2
    return c


def kernel(rows, cols, x_ref, out_ref, peer, own, panel, far, pacc, racc, psrc, pdst, rsrc, rdst,
           ex_sem, ps_sem, pr_sem, zs_sem, zr_sem, xs_sem, xr_sem, qs_sem, qr_sem, ts_sem, tr_sem):
    p, c, l = lax.axis_index("row"), lax.axis_index("col"), lax.axis_index("layer")
    genes, part = x_ref.shape
    half = genes // 2
    samples = 2 * part
    depth = rows // 2
    other = 1 - l

    def remote(src, dst, send, recv, device):
        return pltpu.make_async_remote_copy(
            src_ref=src, dst_ref=dst, send_sem=send, recv_sem=recv, device_id=device, device_id_type=MESH
        )

    barrier = pltpu.get_barrier_semaphore()
    greeted = [(p, c, other)] + [(p, flip(c, k), l) for k in range(1, cols)]
    greeted += [(lax.rem(p + r, rows), c, h) for r in range(1, rows) for h in range(2)]
    for device in greeted:
        pl.semaphore_signal(barrier, inc=1, device_id=device, device_id_type=MESH)
    pl.semaphore_wait(barrier, len(greeted))

    exchange = remote(x_ref, peer, ex_sem.at[0], ex_sem.at[1], (p, c, other))
    exchange.start()
    exchange.wait_recv()

    first = l == 0
    step = 32

    def standardize(h):
        @pl.loop(0, half // step)
        def _(i):
            at = pl.ds(pl.multiple_of(h * half + i * step, step), step)
            mine = x_ref[at, :].astype(jnp.float32)
            theirs = peer[at, :].astype(jnp.float32)
            low = jnp.where(first, mine, theirs)
            high = jnp.where(first, theirs, mine)
            total = jnp.sum(low, axis=1, keepdims=True) + jnp.sum(high, axis=1, keepdims=True)
            squares = jnp.sum(low * low + high * high, axis=1, keepdims=True)
            average = total / samples
            variance = squares / samples - average * average
            gain = lax.rsqrt(variance + epsilon)
            own[at, 0:part] = ((low - average) * gain).astype(jnp.bfloat16)
            own[at, part:samples] = ((high - average) * gain).astype(jnp.bfloat16)

    standardize(l)
    mine_at = pl.ds(pl.multiple_of(l * half, half), half)
    theirs_at = pl.ds(pl.multiple_of(other * half, half), half)

    low_index = lax.rem(p, depth)
    odd = lax.rem(low_index, 2) == 1
    is_low = p < depth
    sends_last = odd == is_low
    receives_last = odd != is_low

    panel_copies = [
        remote(own.at[mine_at], panel.at[c], ps_sem.at[k - 1], pr_sem.at[k - 1], (p, flip(c, k), l))
        for k in range(1, cols)
    ]
    far_copies = [
        remote(own.at[mine_at], far.at[d - 1, mine_at], zs_sem.at[d - 1], zr_sem.at[d - 1],
               (lax.rem(p + d, rows), c, l))
        for d in range(1, depth + 1)
    ]
    for copy in far_copies[:-1]:
        copy.start()
    for copy in panel_copies[:2]:
        copy.start()

    @pl.when(sends_last)
    def _():
        far_copies[-1].start()

    for copy in panel_copies[2:]:
        copy.start()

    standardize(other)
    panel[c] = own[mine_at, :]
    pacc[...] = jnp.zeros_like(pacc)
    racc[...] = jnp.zeros_like(racc)

    def pairs(slot, block, back=None):
        product = lax.dot_general(
            panel[slot], block, (((1,), (1,)), ((), ())), preferred_element_type=jnp.float32
        )
        shifted = product * (0.5 / samples) + 0.5
        square = shifted * shifted
        fourth = square * square
        eighth = fourth * fourth
        value = eighth * fourth
        lanes = value[:, 0:128]
        for j in range(1, genes // 128):
            lanes = lanes + value[:, j * 128:(j + 1) * 128]
        pacc[slot] += lanes
        if back is not None:
            racc[back] += jnp.sum(value.reshape(half // 8, 8, genes), axis=0)

    relays = [
        remote(far.at[d, mine_at], far.at[d, mine_at], xs_sem.at[d], xr_sem.at[d], (p, c, other))
        for d in range(depth)
    ]

    def give_back(d):
        total = racc[d]
        home = lax.rem(p + rows - d - 1, rows)
        for h in range(2):
            rsrc[d, h] = total[:, h * half:(h + 1) * half]
            remote(rsrc.at[d, h], rdst.at[d, l], ts_sem.at[d, h], tr_sem.at[d, l], (home, c, h)).start()

    pairs(c, own[...])
    for k in range(1, cols - 1):
        panel_copies[k - 1].wait_recv()
        pairs(flip(c, k), own[...])
    late = flip(c, cols - 1)
    for d in range(depth - 1):
        far_copies[d].wait_recv()
        relays[d].start()
        relays[d].wait_recv()

        @pl.loop(0, cols - 1)
        def _(j):
            pairs(lax.rem(late + 1 + j, cols), far[d], d)

    @pl.when(receives_last)
    def _():
        far_copies[-1].wait_recv()
        relays[-1].start()

    panel_copies[-1].wait_recv()
    pairs(late, own[...])
    for d in range(depth - 1):
        pairs(late, far[d], d)
        give_back(d)

    @pl.when(receives_last)
    def _():
        relays[-1].wait_recv()

        @pl.loop(0, cols)
        def _(slot):
            pairs(slot, far[depth - 1], depth - 1)

        give_back(depth - 1)

    def fold(slot):
        turned = pacc[slot].T
        return jnp.sum(turned.reshape(128 // 8, 8, half), axis=0)

    part_copies = []
    for k in range(1, cols):
        slot = flip(c, k)
        psrc[k - 1] = fold(slot)
        copy = remote(psrc.at[k - 1], pdst.at[k - 1], qs_sem.at[k - 1], qr_sem.at[k - 1], (p, slot, l))
        copy.start()
        part_copies.append(copy)
    total = fold(c)
    for copy in part_copies:
        copy.wait_recv()
    for k in range(1, cols):
        total = total + pdst[k - 1]

    def back_copy(d, h):
        return remote(rsrc.at[d, h], rdst.at[d, h], ts_sem.at[d, h], tr_sem.at[d, h], (p, c, other))

    for d in range(depth - 1):
        for h in range(2):
            back_copy(d, h).wait_recv()
            total = total + rdst[d, h]
    out_ref[...] = jnp.sum(total, axis=0, keepdims=True) - 1.0

    @pl.when(sends_last)
    def _():
        extra = jnp.zeros_like(total)
        for h in range(2):
            back_copy(depth - 1, h).wait_recv()
            extra = extra + rdst[depth - 1, h]
        out_ref[...] += jnp.sum(extra, axis=0, keepdims=True)
        far_copies[-1].wait_send()

    exchange.wait_send()
    for copy in panel_copies + far_copies[:-1] + relays[:-1] + part_copies:
        copy.wait_send()
    for d in range(depth - 1):
        for h in range(2):
            back_copy(d, h).wait_send()

    @pl.when(receives_last)
    def _():
        relays[-1].wait_send()
        for h in range(2):
            back_copy(depth - 1, h).wait_send()


def solution(mesh):
    rows, cols = mesh.shape["row"], mesh.shape["col"]
    depth = rows // 2
    dma = lambda *shape: pltpu.SemaphoreType.DMA(shape)

    def on_device(expression):
        genes, part = expression.shape
        half, samples = genes // 2, 2 * part
        summed = pl.pallas_call(
            functools.partial(kernel, rows, cols),
            out_shape=jax.ShapeDtypeStruct((1, half), jnp.float32),
            in_specs=[pl.BlockSpec(memory_space=pltpu.VMEM)],
            out_specs=pl.BlockSpec(memory_space=pltpu.VMEM),
            scratch_shapes=[
                pltpu.VMEM((genes, part), jnp.bfloat16),
                pltpu.VMEM((genes, samples), jnp.bfloat16),
                pltpu.VMEM((cols, half, samples), jnp.bfloat16),
                pltpu.VMEM((depth, genes, samples), jnp.bfloat16),
                pltpu.VMEM((cols, half, 128), jnp.float32),
                pltpu.VMEM((depth, 8, genes), jnp.float32),
                pltpu.VMEM((cols - 1, 8, half), jnp.float32),
                pltpu.VMEM((cols - 1, 8, half), jnp.float32),
                pltpu.VMEM((depth, 2, 8, half), jnp.float32),
                pltpu.VMEM((depth, 2, 8, half), jnp.float32),
                dma(2),
                dma(cols - 1), dma(cols - 1),
                dma(depth), dma(depth),
                dma(depth), dma(depth),
                dma(cols - 1), dma(cols - 1),
                dma(depth, 2), dma(depth, 2),
            ],
            compiler_params=pltpu.CompilerParams(collective_id=0, has_side_effects=True),
        )(expression)
        return summed.reshape(half)

    return jax.shard_map(
        on_device,
        mesh=mesh,
        in_specs=(P(("row", "col"), "layer"),),
        out_specs=P(("row", "col", "layer")),
        check_vma=False,
    )
```

time: 121 us -> 36.6 us (0.30)
  waiting for transfers between devices: 83 us -> 0 us
  Pallas kernels: 0 us -> 35.2 us
  blocking collectives: 15.6 us -> 0 us
  between operations: 14.1 us -> 0.02 us
  matrix products: 5.59 us -> 0 us
  other arithmetic: 1.22 us -> 0 us
    all_gather x2 -> x0, waiting for transfers between devices: 82.4 us -> none  [the longest x1 44.6 us: on_device(): row_genes = lax.all_gather(scaled, 'col', axis=0, tiled=True)]
    pallas_call x0 -> x1, Pallas kernels: none -> 35.2 us  [on_device(): pl.pallas_call(functools.partial(kernel, rows, cols), out_shape=jax.Shape...]
    unnamed x1 -> x0, blocking collectives: 12.8 us -> none
    dot_general x1 -> x0, matrix products: 5.59 us -> none  [pair_products(): lax.dot_general(left, right, (((1,), (1,)), ((), ())), preferred_element_...]
    all_gather x1 -> x0, blocking collectives: 2.82 us -> none  [on_device(): whole = lax.all_gather(expression, 'layer', axis=1, tiled=True)]
  transfers between devices with their start and end apart: 2 -> 0, of which waited for: 2 -> 0; matrix products, arithmetic and copies ran while one was open for 0% -> 0% of each run, Pallas kernels for 0% -> 0%
where the time goes in v1:
time: 36.6 us; the launch traced here: 36.5 us
  Pallas kernels  35.2 us (96%)
  local copies, waits for them, and re-layouts  1.22 us (3%)
    pallas_call x1, Pallas kernels, on_device(): pl.pallas_call(functools.partial(kernel, rows, cols), out_shape=jax.Shape...  35.2 us
    unnamed x3, local copies, waits for them, and re-layouts  1.22 us

profile of v1, /device:TPU:0, one launch (start us, length us, event | category | flops | bytes accessed | tf_op | source)
XLA Modules:
  0.0 36.5 jit_solution(14684548847936752916)
XLA Ops:
  0.0 35.2 %shard_map.17 = f32[1,192]{1,0:T(1,128)} custom-call(bf16[384,512]{1,0:T(8,128)(2,1)} %x_ref.1), custom_call_target="tpu_custom_call" | custom-call | tf_op jit(solution)/shard_map/pallas_call | solution.py:223
  35.2 0.0 copy-start
  35.2 0.7 %copy-done = f32[1,192]{1,0:T(1,128)S(1)} copy-done((f32[1,192]{1,0:T(1,128)S(1)}, f32[1,192]{1,0:T(1,128)}, u32[]{:S(2)}) %copy-start) | copy-done | bytes 792
  35.9 0.6 %copy.3 = f32[192]{0:T(256)} copy(f32[192]{0:T(256)S(1)} %bitcast.1) | data formatting | bytes 1536
Async XLA Ops:
  35.2 0.7 %copy-start = (f32[1,192]{1,0:T(1,128)S(1)}, f32[1,192]{1,0:T(1,128)}, u32[]{:S(2)}) copy-start(f32[1,192]{1,0:T(1,128)} %shard_map.17) | copy-start | bytes 2308

commit v2 on v1

v2 whole, which is shorter than its diff:
```python
import functools

import jax
import jax.numpy as jnp
from jax import lax
from jax.experimental import pallas as pl
from jax.experimental.pallas import tpu as pltpu
from jax.sharding import PartitionSpec as P

MESH = pl.DeviceIdType.MESH
epsilon = 1e-05


def flip(c, k):
    bit = 1
    while bit <= k:
        if k & bit:
            c = c + bit - 2 * bit * lax.rem(lax.div(c, bit), 2)
        bit *= 2
    return c


def kernel(rows, cols, x_ref, out_ref, raw, own, panel, far_raw, far, pacc, racc, psrc, pdst, rsrc, rdst,
           in_sem, ex_sem, ps_sem, pr_sem, zs_sem, zr_sem, xs_sem, xr_sem, qs_sem, qr_sem, ts_sem, tr_sem):
    p, c, l = lax.axis_index("row"), lax.axis_index("col"), lax.axis_index("layer")
    genes, part = x_ref.shape
    half = genes // 2
    samples = 2 * part
    depth, pieces, piece = far.shape[0], far.shape[1], far.shape[2]
    other = 1 - l
    late = flip(c, 3)

    def remote(src, dst, send, recv, device):
        return pltpu.make_async_remote_copy(
            src_ref=src, dst_ref=dst, send_sem=send, recv_sem=recv, device_id=device, device_id_type=MESH
        )

    load = pltpu.make_async_copy(x_ref, raw.at[l], in_sem)
    load.start()

    barrier = pltpu.get_barrier_semaphore()
    greeted = [(lax.rem(p + r, rows), c, h) for r in range(1, rows) for h in range(2)]
    greeted += [(p, flip(c, k), l) for k in range(1, cols)] + [(p, c, other)]
    for device in greeted:
        pl.semaphore_signal(barrier, inc=1, device_id=device, device_id_type=MESH)
    pacc[...] = jnp.zeros_like(pacc)
    racc[...] = jnp.zeros_like(racc)
    load.wait()
    pl.semaphore_wait(barrier, len(greeted))

    odd = lax.rem(lax.rem(p, depth), 2) == 1
    is_low = p < depth
    sends_last = odd == is_low
    receives_last = odd != is_low

    def far_copy(d, i):
        at = pl.ds(pl.multiple_of(i * piece, piece), piece)
        return remote(raw.at[l, at], far_raw.at[d, i, l], zs_sem.at[d, i], zr_sem.at[d, i],
                      (lax.rem(p + d + 1, rows), c, l))

    def relay(d, i):
        return remote(far_raw.at[d, i, l], far_raw.at[d, i, l], xs_sem.at[d, i], xr_sem.at[d, i], (p, c, other))

    for d in range(depth - 1):
        for i in range(pieces):
            far_copy(d, i).start()

    @pl.when(sends_last)
    def _():
        for i in range(pieces):
            far_copy(depth - 1, i).start()

    exchange = remote(raw.at[l], raw.at[l], ex_sem.at[0], ex_sem.at[1], (p, c, other))
    exchange.start()
    exchange.wait_recv()

    step = 32

    def scale(low, high):
        low, high = low.astype(jnp.float32), high.astype(jnp.float32)
        total = jnp.sum(low, axis=1, keepdims=True) + jnp.sum(high, axis=1, keepdims=True)
        squares = jnp.sum(low * low + high * high, axis=1, keepdims=True)
        average = total / samples
        variance = squares / samples - average * average
        gain = lax.rsqrt(variance + epsilon)
        return (((low - average) * gain).astype(jnp.bfloat16), ((high - average) * gain).astype(jnp.bfloat16))

    def standardize(h):
        @pl.loop(0, half // step)
        def _(i):
            at = pl.ds(pl.multiple_of(h * half + i * step, step), step)
            low, high = scale(raw[0, at, :], raw[1, at, :])
            own[at, 0:part] = low
            own[at, part:samples] = high

    def standardize_far(d, i):
        @pl.loop(0, piece // step)
        def _(j):
            at = pl.ds(pl.multiple_of(j * step, step), step)
            low, high = scale(far_raw[d, i, 0, at, :], far_raw[d, i, 1, at, :])
            far[d, i, at, 0:part] = low
            far[d, i, at, part:samples] = high

    standardize(l)
    mine_at = pl.ds(pl.multiple_of(l * half, half), half)
    cut = half // 2

    def panel_copy(k, s):
        at = pl.ds(pl.multiple_of(l * half + s * cut, cut), cut)
        return remote(own.at[at], panel.at[c, pl.ds(s * cut, cut)], ps_sem.at[k - 1, s], pr_sem.at[k - 1, s],
                      (p, flip(c, k), l))

    def pass_on(s):
        slot, target = (flip(c, 2), flip(c, 1)) if s == 0 else (flip(c, 1), flip(c, 2))
        at = pl.ds(s * cut, cut)
        return remote(panel.at[slot, at], panel.at[slot, at], ps_sem.at[2, s], pr_sem.at[2, s], (p, target, l))

    direct = [k for k in range(1, cols) if k != 3]
    panel_copies = {(k, s): panel_copy(k, s) for k in direct for s in range(2)}
    panel_copies.update({(3, s): pass_on(s) for s in range(2)})
    for k, s in [(1, 1), (2, 0), (1, 0), (2, 1)] + [(k, s) for k in direct[2:] for s in range(2)]:
        panel_copies[k, s].start()

    standardize(other)
    panel[c] = own[mine_at, :]

    def adjacency(slot, block):
        product = lax.dot_general(
            panel[slot], block, (((1,), (1,)), ((), ())), preferred_element_type=jnp.float32
        )
        shifted = product * (0.5 / samples) + 0.5
        square = shifted * shifted
        fourth = square * square
        eighth = fourth * fourth
        return eighth * fourth

    def own_pairs(slot):
        value = adjacency(slot, own[...])
        lanes = value[:, 0:128]
        for j in range(1, genes // 128):
            lanes = lanes + value[:, j * 128:(j + 1) * 128]
        pacc[slot] += lanes

    def far_pairs(slot, d, i):
        value = adjacency(slot, far[d, i])
        pacc[slot] += value
        racc[d, i] += jnp.sum(value.reshape(half // 8, 8, piece), axis=0)

    count = pieces * jnp.where(receives_last, depth, depth - 1)
    blocks = jnp.where(receives_last, depth, depth - 1)
    mixed = p == 0

    def event(e):
        d = jnp.where(mixed, lax.rem(e, blocks), lax.div(e, pieces))
        i = jnp.where(mixed, lax.div(e, blocks), lax.rem(e, pieces))
        return d, i

    own_pairs(c)
    for s in range(2):
        panel_copies[2 - s, s].wait_recv()
        panel_copies[3, s].start()

    def take(e):
        d, i = event(e)
        far_copy(d, i).wait_recv()
        relay(d, i).start()

    def ready(e):
        d, i = event(e)
        relay(d, i).wait_recv()
        standardize_far(d, i)

    take(0)
    ready(0)
    for s in range(2):
        panel_copies[1 + s, s].wait_recv()
    for k in direct[2:]:
        for s in range(2):
            panel_copies[k, s].wait_recv()
    for k in direct:
        own_pairs(flip(c, k))

    @pl.loop(0, count - 2)
    def _(e):
        @pl.when(e > 0)
        def _():
            take(e)
            ready(e)

        d, i = event(e)

        @pl.loop(0, cols - 1)
        def _(j):
            far_pairs(lax.rem(late + 1 + j, cols), d, i)

    for s in range(2):
        panel_copies[3, s].wait_recv()
    own_pairs(late)

    @pl.loop(0, count - 2)
    def _(e):
        d, i = event(e)
        far_pairs(late, d, i)

    take(count - 2)
    take(count - 1)

    @pl.loop(count - 2, count)
    def _(e):
        ready(e)
        d, i = event(e)

        @pl.loop(0, cols)
        def _(slot):
            far_pairs(slot, d, i)

    def fold(slot):
        turned = pacc[slot].T
        return jnp.sum(turned.reshape(128 // 8, 8, half), axis=0)

    def give_back(d):
        total = jnp.concatenate([racc[d, i] for i in range(pieces)], axis=1)
        home = lax.rem(p + rows - d - 1, rows)
        for h in range(2):
            rsrc[d, h] = total[:, h * half:(h + 1) * half]
            remote(rsrc.at[d, h], rdst.at[d, l], ts_sem.at[d, h], tr_sem.at[d, l], (home, c, h)).start()

    for d in range(depth - 1):
        give_back(d)

    @pl.when(receives_last)
    def _():
        give_back(depth - 1)

    part_copies = []
    for k in range(cols - 1, 0, -1):
        slot = flip(c, k)
        psrc[k - 1] = fold(slot)
        copy = remote(psrc.at[k - 1], pdst.at[k - 1], qs_sem.at[k - 1], qr_sem.at[k - 1], (p, slot, l))
        copy.start()
        part_copies.append(copy)
    total = fold(c)
    for copy in part_copies:
        copy.wait_recv()
    for k in range(1, cols):
        total = total + pdst[k - 1]

    def back_copy(d, h):
        return remote(rsrc.at[d, h], rdst.at[d, h], ts_sem.at[d, h], tr_sem.at[d, h], (p, c, other))

    for d in range(depth - 1):
        for h in range(2):
            back_copy(d, h).wait_recv()
            total = total + rdst[d, h]
    out_ref[...] = total

    @pl.when(sends_last)
    def _():
        extra = jnp.zeros_like(total)
        for h in range(2):
            back_copy(depth - 1, h).wait_recv()
            extra = extra + rdst[depth - 1, h]
        out_ref[...] += extra
        for i in range(pieces):
            far_copy(depth - 1, i).wait_send()

    exchange.wait_send()
    for copy in list(panel_copies.values()) + part_copies:
        copy.wait_send()
    for d in range(depth - 1):
        for i in range(pieces):
            far_copy(d, i).wait_send()
            relay(d, i).wait_send()
        for h in range(2):
            back_copy(d, h).wait_send()

    @pl.when(receives_last)
    def _():
        for i in range(pieces):
            relay(depth - 1, i).wait_send()
        for h in range(2):
            back_copy(depth - 1, h).wait_send()


def solution(mesh):
    rows, cols = mesh.shape["row"], mesh.shape["col"]
    depth = rows // 2
    piece = 128
    dma = lambda *shape: pltpu.SemaphoreType.DMA(shape)

    def on_device(expression):
        genes, part = expression.shape
        half, samples, pieces = genes // 2, 2 * part, genes // piece
        summed = pl.pallas_call(
            functools.partial(kernel, rows, cols),
            out_shape=jax.ShapeDtypeStruct((8, half), jnp.float32),
            in_specs=[pl.BlockSpec(memory_space=pl.ANY)],
            out_specs=pl.BlockSpec(memory_space=pltpu.VMEM),
            scratch_shapes=[
                pltpu.VMEM((2, genes, part), jnp.bfloat16),
                pltpu.VMEM((genes, samples), jnp.bfloat16),
                pltpu.VMEM((cols, half, samples), jnp.bfloat16),
                pltpu.VMEM((depth, pieces, 2, piece, part), jnp.bfloat16),
                pltpu.VMEM((depth, pieces, piece, samples), jnp.bfloat16),
                pltpu.VMEM((cols, half, 128), jnp.float32),
                pltpu.VMEM((depth, pieces, 8, piece), jnp.float32),
                pltpu.VMEM((cols - 1, 8, half), jnp.float32),
                pltpu.VMEM((cols - 1, 8, half), jnp.float32),
                pltpu.VMEM((depth, 2, 8, half), jnp.float32),
                pltpu.VMEM((depth, 2, 8, half), jnp.float32),
                pltpu.SemaphoreType.DMA,
                dma(2),
                dma(cols - 1, 2), dma(cols - 1, 2),
                dma(depth, pieces), dma(depth, pieces),
                dma(depth, pieces), dma(depth, pieces),
                dma(cols - 1), dma(cols - 1),
                dma(depth, 2), dma(depth, 2),
            ],
            compiler_params=pltpu.CompilerParams(collective_id=0, has_side_effects=True),
        )(expression)
        return jnp.sum(summed, axis=0) - 1.0

    return jax.shard_map(
        on_device,
        mesh=mesh,
        in_specs=(P(("row", "col"), "layer"),),
        out_specs=P(("row", "col", "layer")),
        check_vma=False,
    )
```

time: 36.6 us -> 39 us (1.066)
  Pallas kernels: 35.2 us -> 37.6 us
  other arithmetic: 0 us -> 1.28 us
  local copies, waits for them, and re-layouts: 1.22 us -> 0 us
    pallas_call x1, Pallas kernels: 35.2 us -> 37.6 us  [on_device(): pl.pallas_call(functools.partial(kernel, rows, cols), out_shape=jax.Shape...]
    unnamed x3 -> x0, local copies, waits for them, and re-layouts: 1.22 us -> none
    reduce_sum x0 -> x1, other arithmetic: none -> 0.72 us  [on_device(): return jnp.sum(summed, axis=0) - 1.0]
    sub x0 -> x1, other arithmetic: none -> 0.57 us  [on_device(): return jnp.sum(summed, axis=0) - 1.0]
where the time goes in v2:
time: 39 us; the launch traced here: 38.8 us
  Pallas kernels  37.6 us (96%)
  other arithmetic  1.28 us (3%)
    pallas_call x1, Pallas kernels, on_device(): pl.pallas_call(functools.partial(kernel, rows, cols), out_shape=jax.Shape...  37.6 us

profile of v2, /device:TPU:0, one launch (start us, length us, event | category | flops | bytes accessed | tf_op | source)
XLA Modules:
  0.0 38.8 jit_solution(7459733221550148792)
XLA Ops:
  0.0 37.6 %shard_map.17 = f32[8,192]{1,0:T(8,128)} custom-call(bf16[384,512]{1,0:T(8,128)(2,1)} %x_ref.1), custom_call_target="tpu_custom_call" | custom-call | tf_op jit(solution)/shard_map/pallas_call | solution.py:294
  37.6 0.7 %reduce_sum.9 = f32[192]{0:T(256)S(1)} reduce(f32[8,192]{1,0:T(8,128)} %shard_map.17, f32[]{:T(128)} %constant.1.clone.1), dimensions={0}, to_apply=%region_0.0 | reduce | flops 1344 | bytes 6916 | tf_op jit(solution)/shard_map/reduce_sum | solution.py:321
  38.3 0.6 %broadcast_add_fusion = f32[192]{0:T(256)} fusion(f32[192]{0:T(256)S(1)} %reduce_sum.9), kind=kLoop, calls=%fused_computation | loop fusion | flops 192 | bytes 1536 | tf_op jit(solution)/shard_map/sub | solution.py:321

commit v3 on v2

--- a/solution.py
+++ b/solution.py
@@ -28,7 +28,11 @@
     samples = 2 * part
     depth, pieces, piece = far.shape[0], far.shape[1], far.shape[2]
     other = 1 - l
-    late = flip(c, 3)
+    order = [k for k in range(cols) if k != 3] + [3]
+    last = cols - 1
+
+    def rows_of(first, stop):
+        return pl.ds(first * half, (stop - first) * half)
 
     def remote(src, dst, send, recv, device):
         return pltpu.make_async_remote_copy(
@@ -107,13 +111,13 @@
 
     def panel_copy(k, s):
         at = pl.ds(pl.multiple_of(l * half + s * cut, cut), cut)
-        return remote(own.at[at], panel.at[c, pl.ds(s * cut, cut)], ps_sem.at[k - 1, s], pr_sem.at[k - 1, s],
+        return remote(own.at[at], panel.at[pl.ds(order.index(k) * half + s * cut, cut)], ps_sem.at[k - 1, s], pr_sem.at[k - 1, s],
                       (p, flip(c, k), l))
 
     def pass_on(s):
-        slot, target = (flip(c, 2), flip(c, 1)) if s == 0 else (flip(c, 1), flip(c, 2))
-        at = pl.ds(s * cut, cut)
-        return remote(panel.at[slot, at], panel.at[slot, at], ps_sem.at[2, s], pr_sem.at[2, s], (p, target, l))
+        source, target = (2, 1) if s == 0 else (1, 2)
+        return remote(panel.at[pl.ds(source * half + s * cut, cut)], panel.at[pl.ds(last * half + s * cut, cut)],
+                      ps_sem.at[2, s], pr_sem.at[2, s], (p, flip(c, target), l))
 
     direct = [k for k in range(1, cols) if k != 3]
     panel_copies = {(k, s): panel_copy(k, s) for k in direct for s in range(2)}
@@ -122,11 +126,11 @@
         panel_copies[k, s].start()
 
     standardize(other)
-    panel[c] = own[mine_at, :]
-
-    def adjacency(slot, block):
+    panel[rows_of(0, 1), :] = own[mine_at, :]
+
+    def adjacency(at, block):
         product = lax.dot_general(
-            panel[slot], block, (((1,), (1,)), ((), ())), preferred_element_type=jnp.float32
+            panel[at, :], block, (((1,), (1,)), ((), ())), preferred_element_type=jnp.float32
         )
         shifted = product * (0.5 / samples) + 0.5
         square = shifted * shifted
@@ -134,17 +138,20 @@
         eighth = fourth * fourth
         return eighth * fourth
 
-    def own_pairs(slot):
-        value = adjacency(slot, own[...])
+    def own_pairs(first, stop):
+        at = rows_of(first, stop)
+        value = adjacency(at, own[...])
         lanes = value[:, 0:128]
         for j in range(1, genes // 128):
             lanes = lanes + value[:, j * 128:(j + 1) * 128]
-        pacc[slot] += lanes
-
-    def far_pairs(slot, d, i):
-        value = adjacency(slot, far[d, i])
-        pacc[slot] += value
-        racc[d, i] += jnp.sum(value.reshape(half // 8, 8, piece), axis=0)
+        pacc[at, :] += lanes
+
+    def far_pairs(first, stop, e):
+        d, i = event(e)
+        at = rows_of(first, stop)
+        value = adjacency(at, far[d, i])
+        pacc[at, :] += value
+        racc[d, i] += jnp.sum(value.reshape(value.shape[0] // 8, 8, piece), axis=0)
 
     count = pieces * jnp.where(receives_last, depth, depth - 1)
     blocks = jnp.where(receives_last, depth, depth - 1)
@@ -155,7 +162,7 @@
         i = jnp.where(mixed, lax.div(e, blocks), lax.rem(e, pieces))
         return d, i
 
-    own_pairs(c)
+    own_pairs(0, 1)
     for s in range(2):
         panel_copies[2 - s, s].wait_recv()
         panel_copies[3, s].start()
@@ -171,51 +178,55 @@
         standardize_far(d, i)
 
     take(0)
+    take(1)
     ready(0)
+    take(2)
+    ready(1)
     for s in range(2):
         panel_copies[1 + s, s].wait_recv()
     for k in direct[2:]:
         for s in range(2):
             panel_copies[k, s].wait_recv()
-    for k in direct:
-        own_pairs(flip(c, k))
+    own_pairs(1, last)
+    longer = count > 3
+
+    @pl.when(longer)
+    def _():
+        take(3)
 
     @pl.loop(0, count - 2)
     def _(e):
-        @pl.when(e > 0)
+        @pl.when(e > 1)
         def _():
-            take(e)
+            @pl.when(e > 3)
+            def _():
+                take(e)
+
             ready(e)
 
-        d, i = event(e)
-
-        @pl.loop(0, cols - 1)
-        def _(j):
-            far_pairs(lax.rem(late + 1 + j, cols), d, i)
+        far_pairs(0, last, e)
 
     for s in range(2):
         panel_copies[3, s].wait_recv()
-    own_pairs(late)
+    own_pairs(last, cols)
 
     @pl.loop(0, count - 2)
     def _(e):
-        d, i = event(e)
-        far_pairs(late, d, i)
-
-    take(count - 2)
-    take(count - 1)
-
-    @pl.loop(count - 2, count)
-    def _(e):
-        ready(e)
-        d, i = event(e)
-
-        @pl.loop(0, cols)
-        def _(slot):
-            far_pairs(slot, d, i)
-
-    def fold(slot):
-        turned = pacc[slot].T
+        far_pairs(last, cols, e)
+
+    @pl.when(longer)
+    def _():
+        take(count - 2)
+        take(count - 1)
+        ready(count - 2)
+
+    far_pairs(0, cols, count - 2)
+    ready(count - 1)
+    far_pairs(0, cols, count - 1)
+
+    def fold(k):
+        at = order.index(k)
+        turned = pacc[rows_of(at, at + 1), :].T
         return jnp.sum(turned.reshape(128 // 8, 8, half), axis=0)
 
     def give_back(d):
@@ -234,12 +245,11 @@
 
     part_copies = []
     for k in range(cols - 1, 0, -1):
-        slot = flip(c, k)
-        psrc[k - 1] = fold(slot)
-        copy = remote(psrc.at[k - 1], pdst.at[k - 1], qs_sem.at[k - 1], qr_sem.at[k - 1], (p, slot, l))
+        psrc[k - 1] = fold(k)
+        copy = remote(psrc.at[k - 1], pdst.at[k - 1], qs_sem.at[k - 1], qr_sem.at[k - 1], (p, flip(c, k), l))
         copy.start()
         part_copies.append(copy)
-    total = fold(c)
+    total = fold(0) - 1.0 / 8
     for copy in part_copies:
         copy.wait_recv()
     for k in range(1, cols):
@@ -299,10 +309,10 @@
             scratch_shapes=[
                 pltpu.VMEM((2, genes, part), jnp.bfloat16),
                 pltpu.VMEM((genes, samples), jnp.bfloat16),
-                pltpu.VMEM((cols, half, samples), jnp.bfloat16),
+                pltpu.VMEM((cols * half, samples), jnp.bfloat16),
                 pltpu.VMEM((depth, pieces, 2, piece, part), jnp.bfloat16),
                 pltpu.VMEM((depth, pieces, piece, samples), jnp.bfloat16),
-                pltpu.VMEM((cols, half, 128), jnp.float32),
+                pltpu.VMEM((cols * half, 128), jnp.float32),
                 pltpu.VMEM((depth, pieces, 8, piece), jnp.float32),
                 pltpu.VMEM((cols - 1, 8, half), jnp.float32),
                 pltpu.VMEM((cols - 1, 8, half), jnp.float32),
@@ -318,7 +328,7 @@
             ],
             compiler_params=pltpu.CompilerParams(collective_id=0, has_side_effects=True),
         )(expression)
-        return jnp.sum(summed, axis=0) - 1.0
+        return jnp.sum(summed, axis=0)
 
     return jax.shard_map(
         on_device,

time: 39 us -> 35.5 us (0.910)
  Pallas kernels: 37.6 us -> 34 us
    pallas_call x1, Pallas kernels: 37.6 us -> 34 us  [on_device(): pl.pallas_call(functools.partial(kernel, rows, cols), out_shape=jax.Shape...]
    sub x1 -> x0, other arithmetic: 0.57 us -> none  [on_device(): return jnp.sum(summed, axis=0) - 1.0]
    reduce_sum x1, other arithmetic: 0.72 us -> 1.28 us  [on_device(): return jnp.sum(summed, axis=0)]
where the time goes in v3:
time: 35.5 us; the launch traced here: 35.3 us
  Pallas kernels  34 us (96%)
  other arithmetic  1.28 us (4%)
    pallas_call x1, Pallas kernels, on_device(): pl.pallas_call(functools.partial(kernel, rows, cols), out_shape=jax.Shape...  34 us
    reduce_sum x1, other arithmetic, on_device(): return jnp.sum(summed, axis=0)  1.28 us

profile of v3, /device:TPU:0, one launch (start us, length us, event | category | flops | bytes accessed | tf_op | source)
XLA Modules:
  0.0 35.3 jit_solution(13015778420908486705)
XLA Ops:
  0.0 34.0 %shard_map.17 = f32[8,192]{1,0:T(8,128)} custom-call(bf16[384,512]{1,0:T(8,128)(2,1)} %x_ref.1), custom_call_target="tpu_custom_call" | custom-call | tf_op jit(solution)/shard_map/pallas_call | solution.py:304
  34.0 1.3 %reduce_sum.9 = f32[192]{0:T(256)} reduce(f32[8,192]{1,0:T(8,128)} %shard_map.17, f32[]{:T(128)} %constant.0.clone.1), dimensions={0}, to_apply=%region_0.0 | reduce | flops 1344 | bytes 6916 | tf_op jit(solution)/shard_map/reduce_sum | solution.py:331

commit v4 on v3

--- a/solution.py
+++ b/solution.py
@@ -90,17 +90,15 @@
         return (((low - average) * gain).astype(jnp.bfloat16), ((high - average) * gain).astype(jnp.bfloat16))
 
     def standardize(h):
-        @pl.loop(0, half // step)
-        def _(i):
+        for i in range(half // step):
             at = pl.ds(pl.multiple_of(h * half + i * step, step), step)
             low, high = scale(raw[0, at, :], raw[1, at, :])
             own[at, 0:part] = low
             own[at, part:samples] = high
 
     def standardize_far(d, i):
-        @pl.loop(0, piece // step)
-        def _(j):
-            at = pl.ds(pl.multiple_of(j * step, step), step)
+        for j in range(piece // step):
+            at = pl.ds(j * step, step)
             low, high = scale(far_raw[d, i, 0, at, :], far_raw[d, i, 1, at, :])
             far[d, i, at, 0:part] = low
             far[d, i, at, part:samples] = high
@@ -154,13 +152,9 @@
         racc[d, i] += jnp.sum(value.reshape(value.shape[0] // 8, 8, piece), axis=0)
 
     count = pieces * jnp.where(receives_last, depth, depth - 1)
-    blocks = jnp.where(receives_last, depth, depth - 1)
-    mixed = p == 0
 
     def event(e):
-        d = jnp.where(mixed, lax.rem(e, blocks), lax.div(e, pieces))
-        i = jnp.where(mixed, lax.div(e, blocks), lax.rem(e, pieces))
-        return d, i
+        return lax.div(e, pieces), lax.rem(e, pieces)
 
     own_pairs(0, 1)
     for s in range(2):
@@ -178,8 +172,8 @@
         standardize_far(d, i)
 
     take(0)
+    ready(0)
     take(1)
-    ready(0)
     take(2)
     ready(1)
     for s in range(2):
@@ -220,9 +214,11 @@
         take(count - 1)
         ready(count - 2)
 
-    far_pairs(0, cols, count - 2)
+    far_pairs(0, last, count - 2)
+    far_pairs(last, cols, count - 2)
     ready(count - 1)
-    far_pairs(0, cols, count - 1)
+    far_pairs(0, last, count - 1)
+    far_pairs(last, cols, count - 1)
 
     def fold(k):
         at = order.index(k)
@@ -262,7 +258,8 @@
         for h in range(2):
             back_copy(d, h).wait_recv()
             total = total + rdst[d, h]
-    out_ref[...] = total
+
+    out_ref[...] = jnp.sum(total, axis=0)
 
     @pl.when(sends_last)
     def _():
@@ -270,7 +267,7 @@
         for h in range(2):
             back_copy(depth - 1, h).wait_recv()
             extra = extra + rdst[depth - 1, h]
-        out_ref[...] += extra
+        out_ref[...] += jnp.sum(extra, axis=0)
         for i in range(pieces):
             far_copy(depth - 1, i).wait_send()
 
@@ -303,7 +300,7 @@
         half, samples, pieces = genes // 2, 2 * part, genes // piece
         summed = pl.pallas_call(
             functools.partial(kernel, rows, cols),
-            out_shape=jax.ShapeDtypeStruct((8, half), jnp.float32),
+            out_shape=jax.ShapeDtypeStruct((half,), jnp.float32),
             in_specs=[pl.BlockSpec(memory_space=pl.ANY)],
             out_specs=pl.BlockSpec(memory_space=pltpu.VMEM),
             scratch_shapes=[
@@ -328,7 +325,7 @@
             ],
             compiler_params=pltpu.CompilerParams(collective_id=0, has_side_effects=True),
         )(expression)
-        return jnp.sum(summed, axis=0)
+        return summed
 
     return jax.shard_map(
         on_device,

time: 35.5 us -> 32.3 us (0.910)
  Pallas kernels: 34 us -> 30.9 us
  other arithmetic: 1.28 us -> 0 us
  local copies, waits for them, and re-layouts: 0 us -> 1.24 us
    pallas_call x1, Pallas kernels: 34 us -> 30.9 us  [on_device(): pl.pallas_call(functools.partial(kernel, rows, cols), out_shape=jax.Shape...]
    reduce_sum x1 -> x0, other arithmetic: 1.28 us -> none  [on_device(): return jnp.sum(summed, axis=0)]
    unnamed x0 -> x1, local copies, waits for them, and re-layouts: none -> 1.24 us
where the time goes in v4:
time: 32.3 us; the launch traced here: 32.1 us
  Pallas kernels  30.9 us (96%)
  local copies, waits for them, and re-layouts  1.24 us (4%)
    pallas_call x1, Pallas kernels, on_device(): pl.pallas_call(functools.partial(kernel, rows, cols), out_shape=jax.Shape...  30.9 us
    unnamed x1, local copies, waits for them, and re-layouts  1.24 us

profile of v4, /device:TPU:0, one launch (start us, length us, event | category | flops | bytes accessed | tf_op | source)
XLA Modules:
  0.0 32.1 jit_solution(6338765448054986819)
XLA Ops:
  0.0 30.9 %shard_map.17 = f32[192]{0:T(256)} custom-call(bf16[384,512]{1,0:T(8,128)(2,1)} %x_ref.1), custom_call_target="tpu_custom_call" | custom-call | tf_op jit(solution)/shard_map/pallas_call | solution.py:301
  30.9 1.2 %copy.3 = f32[192]{0:T(256)} copy(f32[192]{0:T(256)} %shard_map.17) | data formatting | bytes 1536
